TPU v7x, 32 devices: a whole 2x2x4 slice. The times are simulated.
32 devices in a mesh: dp: 16 (over z, y, core), tensor: 2 (over x).
Axes of the slice: x: 2, y: 2, z: 4, core: 2. Of those that a mesh axis runs over, the one named last changes fastest.
Arguments:
- step: int32 [1], replicated, may hold values from 0 to 999
- activations: bfloat16 [2, 16384, 8192], P(None, 'dp', 'tensor'), may hold values from -6 to 6
- grad_weight: bfloat16 [2, 8192, 28672], P(None, 'tensor', 'dp'), may hold values from -6 to 6
Outputs:
- preconditioned: float32 [8192, 28672], P('tensor', 'dp')
All inputs are finite; a program needn't handle non-finite values.
Results may differ from a plain program's by a relative error of at most 0.0044.
Values may be sent and summed in bfloat16 or wider, within the bound.
No kernel may reach another device: no remote copies, remote signals or barrier semaphores. Data moves between devices by JAX's collectives and lax.ppermute only.
A program may use at most 192 MiB of HBM per device.

v0:
```python
import jax
import jax.numpy as jnp
from jax import lax
from jax.sharding import PartitionSpec as P

BLOCK = 1024
LAYERS = 2
ITERS = 4


def local(step, activations, grad_weight):
    groups = lax.axis_size("dp")
    layer = step[0] % LAYERS
    damping = 0.05 + 0.1 * step[0].astype(jnp.float32) / 1000.0
    acts = lax.dynamic_index_in_dim(activations, layer, 0, keepdims=False)
    grads = lax.dynamic_index_in_dim(grad_weight, layer, 0, keepdims=False)
    tok_rows = acts.shape[0]
    width = acts.shape[1]
    nblock = width // BLOCK
    share = BLOCK // groups
    blocks = acts.reshape(tok_rows, nblock, BLOCK)
    total_tokens = tok_rows * groups
    first = lax.axis_index("dp") * share
    summed = lax.psum(
        jnp.einsum("tkr,tkc->rkc", blocks, blocks, preferred_element_type=jnp.float32), "dp"
    )
    gram_rows = lax.dynamic_slice_in_dim(summed, first, share, 0)
    row_ids = first + lax.broadcasted_iota(jnp.int32, (share, 1, BLOCK), 0)
    col_ids = lax.broadcasted_iota(jnp.int32, (share, 1, BLOCK), 2)
    identity = (row_ids == col_ids).astype(jnp.float32)
    factor = gram_rows / total_tokens + damping * identity
    block_squares = lax.psum(jnp.sum(factor * factor, axis=(0, 2)), "dp")
    largest = lax.pmax(jnp.max(block_squares), "tensor")
    iterate = jnp.broadcast_to(identity / jnp.sqrt(largest), factor.shape)
    for sweep in range(ITERS):
        whole = lax.all_gather(iterate, "dp", axis=0, tiled=True)
        product = jnp.einsum("rkj,jkc->rkc", factor, whole, precision=lax.Precision.HIGHEST)
        iterate = 2.0 * iterate - jnp.einsum(
            "rkj,jkc->rkc", product, whole, precision=lax.Precision.HIGHEST
        )
    inverse = iterate.astype(jnp.bfloat16)
    stacked = grads.reshape(nblock, BLOCK, grads.shape[1])
    result = jnp.einsum(
        "rkc,kcf->krf",
        lax.all_gather(inverse, "dp", axis=0, tiled=True),
        stacked,
        preferred_element_type=jnp.float32,
    )
    return result.reshape(width, grads.shape[1])


def solution(mesh):
    in_specs = (P(), P(None, "dp", "tensor"), P(None, "tensor", "dp"))
    out_specs = P("tensor", "dp")
    return jax.shard_map(local, mesh=mesh, in_specs=in_specs, out_specs=out_specs, check_vma=False)
```

profile of v0, /device:TPU:0, one launch (start us, length us, event | category | flops | bytes accessed | tf_op | source)
XLA Modules:
  0.0 1019.5 jit_solution(3891566731821359104)
XLA Ops:
  6.5 0.0 all-reduce.2.cloned.1.call-start
  7.2 7.9 constant_dynamic-slice_fusion.1
  15.1 12.0 %copy.23 = bf16[1,1024,4096]{1,2,0:T(8,128)(2,1)} copy(bf16[1,1024,4096]{2,1,0:T(8,128)(2,1)} %constant_dynamic-slice_fusion.1) | data formatting | bytes 16777216
  27.1 17.1 %convolution_bitcast_fusion = f32[1024,4,1024]{2,0,1:T(8,128)} fusion(bf16[1024,4,1024]{0,2,1:T(8,128)(2,1)} %bitcast.51), kind=kOutput, calls=%fused_computation | convolution fusion | flops 8589934592 | bytes 25165824 | tf_op jit(solution)/shard_map/tkr,tkc->rkc/dot_general | solution.py:25
  44.2 0.0 all-reduce.2.cloned.1.call-update
  44.3 0.0 all-gather.14.cloned.1.call-start
  44.3 0.1 fusion.18
  44.4 300.7 %all-reduce.2.cloned.1.call-done = f32[1024,4,1024]{2,0,1:T(8,128)} async-done(((f32[1024,4,1024]{2,0,1:T(8,128)}), f32[1024,4,1024]{2,0,1:T(8,128)}) %all-reduce.2.cloned.1.call-update) | async-done | bytes 16777232 | tf_op jit(solution)/shard_map/psum | solution.py:24
  345.1 1.5 multiply_reduce_fusion
  346.6 31.8 %psum.15 = f32[4]{0:T(128)S(1)} all-reduce(f32[4]{0:T(128)S(1)} %multiply_reduce_fusion), channel_id=1, replica_groups=mesh['dp'=16,'tensor'=2] {'dp'}, use_global_device_ids=true, to_apply=%region_2.3 | all-reduce | flops 4 | bytes 32 | tf_op jit(solution)/shard_map/psum | solution.py:32
  378.4 0.6 reduce_max.9
  379.0 5.5 pmax.7
  385.2 0.8 broadcast_multiply_fusion
  386.0 0.0 all-gather.14.cloned.1.call-update
  386.0 0.3 all-gather.6.cloned.1.call-start
  386.3 47.5 %all-gather.14.cloned.1.call-done = f32[1024,1024]{1,0:T(8,128)} async-done(((f32[64,1024]{1,0:T(8,128)}), f32[1024,1024]{1,0:T(8,128)}) %all-gather.14.cloned.1.call-update) | async-done | bytes 4194320 | tf_op jit(solution)/shard_map/all_gather | solution.py:36
  433.8 11.8 %fusion.4 = f32[64,4,1024]{2,0,1:T(8,128)S(1)} fusion(f32[1024,1024]{1,0:T(8,128)} %all-gather.14.cloned.1.call-done, f32[1024,4,1024]{2,0,1:T(8,128)} %all-reduce.2.cloned.1.call-done, s32[]{:T(128)S(6)} %select_n.18, f32[64,1024]{1,0:T(8,128)S(1)} %fusion.18), kind=kOutput, calls=%fused_computation.5 | convolution fusion | flops 3221749760 | bytes 6553604 | tf_op jit(solution)/shard_map/rkj,jkc->rkc/dot_general | solution.py:37
  445.6 12.8 %fusion.10 = f32[64,4,1024]{2,0,1:T(8,128)} fusion(f32[64,4,1024]{2,0,1:T(8,128)S(1)} %fusion.4, f32[1024,1024]{1,0:T(8,128)} %all-gather.14.cloned.1.call-done, f32[64,1024]{1,0:T(8,128)S(1)} %get-tuple-element.5), kind=kOutput, calls=%fused_computation.7 | convolution fusion | flops 3221487616 | bytes 6553600 | tf_op jit(solution)/shard_map/rkj,jkc->rkc/dot_general | solution.py:38
  458.3 0.0 copy-start.4
  458.3 0.0 all-gather.6.cloned.1.call-update
  458.4 0.0 all-gather.8.cloned.1.call-start
  458.4 125.1 %all-gather.6.cloned.1.call-done = f32[1024,4,1024]{2,0,1:T(8,128)} async-done(((f32[64,4,1024]{2,0,1:T(8,128)}), f32[1024,4,1024]{2,0,1:T(8,128)}) %all-gather.6.cloned.1.call-update) | async-done | bytes 16777232 | tf_op jit(solution)/shard_map/all_gather | solution.py:36
  583.5 0.0 copy-start.1
  583.5 15.3 %convolution_bitcast_fusion.6 = f32[64,4,1024]{2,0,1:T(8,128)S(1)} fusion(f32[1024,4,1024]{2,0,1:T(8,128)} %all-gather.6.cloned.1.call-done, f32[1024,4,1024]{2,0,1:T(8,128)} %all-reduce.2.cloned.1.call-done, s32[]{:T(128)S(6)} %select_n.18, f32[64,1024]{1,0:T(8,128)S(1)} %fusion.18), kind=kOutput, calls=%fused_computation.16 | convolution fusion | flops 3221749760 | bytes 19136516 | tf_op jit(solution)/shard_map/rkj,jkc->rkc/dot_general | solution.py:37
  598.8 0.0 copy-done.4
  598.8 0.0 copy-done.1
  598.8 11.8 %fusion.15 = f32[64,4,1024]{2,0,1:T(8,128)} fusion(f32[1024,4,1024]{2,0,1:T(8,128)S(1)} %copy-done.1, f32[64,4,1024]{2,0,1:T(8,128)S(1)} %convolution_bitcast_fusion.6, f32[64,4,1024]{2,0,1:T(8,128)S(1)} %copy-done.4), kind=kOutput, calls=%fused_computation.15 | convolution fusion | flops 3221749760 | bytes 19922944 | tf_op jit(solution)/shard_map/rkj,jkc->rkc/dot_general | solution.py:38
  610.6 0.0 copy-start.5
  610.6 0.0 all-gather.8.cloned.1.call-update
  610.6 0.0 all-gather.10.cloned.1.call-start
  610.7 124.7 %all-gather.8.cloned.1.call-done = f32[1024,4,1024]{2,0,1:T(8,128)} async-done(((f32[64,4,1024]{2,0,1:T(8,128)}), f32[1024,4,1024]{2,0,1:T(8,128)}) %all-gather.8.cloned.1.call-update) | async-done | bytes 16777232 | tf_op jit(solution)/shard_map/all_gather | solution.py:36
  735.4 0.0 copy-start.2
  735.4 15.0 %convolution_bitcast_fusion.4 = f32[64,4,1024]{2,0,1:T(8,128)S(1)} fusion(f32[1024,4,1024]{2,0,1:T(8,128)} %all-gather.8.cloned.1.call-done, f32[1024,4,1024]{2,0,1:T(8,128)} %all-reduce.2.cloned.1.call-done, s32[]{:T(128)S(6)} %select_n.18, f32[64,1024]{1,0:T(8,128)S(1)} %fusion.18), kind=kOutput, calls=%fused_computation.13 | convolution fusion | flops 3221749760 | bytes 19136516 | tf_op jit(solution)/shard_map/rkj,jkc->rkc/dot_general | solution.py:37
  750.4 0.0 copy-done.5
  750.4 0.0 copy-done.2
  750.4 11.8 %fusion.14 = f32[64,4,1024]{2,0,1:T(8,128)} fusion(f32[1024,4,1024]{2,0,1:T(8,128)S(1)} %copy-done.2, f32[64,4,1024]{2,0,1:T(8,128)S(1)} %convolution_bitcast_fusion.4, f32[64,4,1024]{2,0,1:T(8,128)S(1)} %copy-done.5), kind=kOutput, calls=%fused_computation.12 | convolution fusion | flops 3221749760 | bytes 19922944 | tf_op jit(solution)/shard_map/rkj,jkc->rkc/dot_general | solution.py:38
  762.2 0.0 copy-start.3
  762.2 0.0 all-gather.10.cloned.1.call-update
  762.2 0.0 all-gather.12.cloned.1.call-start
  762.3 124.7 %all-gather.10.cloned.1.call-done = f32[1024,4,1024]{2,0,1:T(8,128)} async-done(((f32[64,4,1024]{2,0,1:T(8,128)}), f32[1024,4,1024]{2,0,1:T(8,128)}) %all-gather.10.cloned.1.call-update) | async-done | bytes 16777232 | tf_op jit(solution)/shard_map/all_gather | solution.py:36
  887.0 0.0 copy-start
  887.0 15.0 %convolution_bitcast_fusion.2 = f32[64,4,1024]{2,0,1:T(8,128)S(1)} fusion(f32[1024,4,1024]{2,0,1:T(8,128)} %all-gather.10.cloned.1.call-done, f32[1024,4,1024]{2,0,1:T(8,128)} %all-reduce.2.cloned.1.call-done, s32[]{:T(128)S(6)} %select_n.18, f32[64,1024]{1,0:T(8,128)S(1)} %fusion.18), kind=kOutput, calls=%fused_computation.10 | convolution fusion | flops 3221749760 | bytes 19136516 | tf_op jit(solution)/shard_map/rkj,jkc->rkc/dot_general | solution.py:37
  902.0 0.0 copy-done.3
  902.0 0.0 copy-done
  902.0 11.6 %fusion.16 = bf16[64,4,1024]{2,0,1:T(8,128)(2,1)} fusion(f32[1024,4,1024]{2,0,1:T(8,128)S(1)} %copy-done, f32[64,4,1024]{2,0,1:T(8,128)S(1)} %convolution_bitcast_fusion.2, f32[64,4,1024]{2,0,1:T(8,128)S(1)} %copy-done.3), kind=kOutput, calls=%fused_computation.17 | convolution fusion | flops 3222011904 | bytes 19398656 | tf_op jit(solution)/shard_map/rkj,jkc->rkc/dot_general | solution.py:38
  913.7 0.0 all-gather.12.cloned.1.call-update
  913.7 13.2 %constant_dynamic-slice_fusion = bf16[1,4096,1792]{2,1,0:T(8,128)(2,1)} fusion(bf16[2,4096,1792]{2,1,0:T(8,128)(2,1)} %param.5, s32[]{:T(128)S(6)} %select_n.17), kind=kLoop, calls=%fused_computation.24 | loop fusion | bytes 29360132 | tf_op jit(solution)/shard_map/jit(dynamic_index_in_dim)/dynamic_slice | solution.py:16
  926.9 59.4 %all-gather.12.cloned.1.call-done = bf16[1024,4,1024]{2,0,1:T(8,128)(2,1)} async-done(((bf16[64,4,1024]{2,0,1:T(8,128)(2,1)}), bf16[1024,4,1024]{2,0,1:T(8,128)(2,1)}) %all-gather.12.cloned.1.call-update) | async-done | bytes 8388624 | tf_op jit(solution)/shard_map/all_gather | solution.py:45
  986.3 25.9 %fusion.19 = f32[4,1024,1792]{2,1,0:T(8,128)} fusion(bf16[1024,4,1024]{2,0,1:T(8,128)(2,1)} %all-gather.12.cloned.1.call-done, bf16[4,1024,1792]{2,1,0:T(8,128)(2,1)} %bitcast.50), kind=kOutput, calls=%fused_computation.27 | convolution fusion | flops 15032385536 | bytes 52428800 | tf_op jit(solution)/shard_map/rkc,kcf->krf/dot_general | solution.py:43
  (1 shorter events, 0.0 us)
Async XLA Ops:
  6.5 338.6 %all-reduce.2.cloned.1.call-start = ((), (), s32[]{:S(2)}) async-start(), calls=%async_computation | async-start | bytes 33554432 | tf_op jit(solution)/shard_map/psum | solution.py:24
  44.3 389.5 %all-gather.14.cloned.1.call-start = ((), (), s32[]{:S(2)}) async-start(), calls=%async_computation.5 | async-start | bytes 4456448 | tf_op jit(solution)/shard_map/all_gather | solution.py:36
  386.0 197.5 %all-gather.6.cloned.1.call-start = ((), (), s32[]{:S(2)}) async-start(), calls=%async_computation.1 | async-start | bytes 17825792 | tf_op jit(solution)/shard_map/all_gather | solution.py:36
  458.3 140.4 %copy-start.4 = (f32[64,4,1024]{2,0,1:T(8,128)S(1)}, f32[64,4,1024]{2,0,1:T(8,128)}, u32[]{:S(2)}) copy-start(f32[64,4,1024]{2,0,1:T(8,128)} %fusion.10) | copy-start | bytes 3145732
  458.4 277.0 %all-gather.8.cloned.1.call-start = ((), (), s32[]{:S(2)}) async-start(), calls=%async_computation.2 | async-start | bytes 17825792 | tf_op jit(solution)/shard_map/all_gather | solution.py:36
  583.5 15.3 %copy-start.1 = (f32[1024,4,1024]{2,0,1:T(8,128)S(1)}, f32[1024,4,1024]{2,0,1:T(8,128)}, u32[]{:S(2)}) copy-start(f32[1024,4,1024]{2,0,1:T(8,128)} %all-gather.6.cloned.1.call-done) | copy-start | bytes 50331652
  610.6 139.8 %copy-start.5 = (f32[64,4,1024]{2,0,1:T(8,128)S(1)}, f32[64,4,1024]{2,0,1:T(8,128)}, u32[]{:S(2)}) copy-start(f32[64,4,1024]{2,0,1:T(8,128)} %fusion.15) | copy-start | bytes 3145732
  610.6 276.4 %all-gather.10.cloned.1.call-start = ((), (), s32[]{:S(2)}) async-start(), calls=%async_computation.3 | async-start | bytes 17825792 | tf_op jit(solution)/shard_map/all_gather | solution.py:36
  735.4 15.0 %copy-start.2 = (f32[1024,4,1024]{2,0,1:T(8,128)S(1)}, f32[1024,4,1024]{2,0,1:T(8,128)}, u32[]{:S(2)}) copy-start(f32[1024,4,1024]{2,0,1:T(8,128)} %all-gather.8.cloned.1.call-done) | copy-start | bytes 50331652
  762.2 139.8 %copy-start.3 = (f32[64,4,1024]{2,0,1:T(8,128)S(1)}, f32[64,4,1024]{2,0,1:T(8,128)}, u32[]{:S(2)}) copy-start(f32[64,4,1024]{2,0,1:T(8,128)} %fusion.14) | copy-start | bytes 3145732
  762.2 224.1 %all-gather.12.cloned.1.call-start = ((), (), s32[]{:S(2)}) async-start(), calls=%async_computation.4 | async-start | bytes 8912896 | tf_op jit(solution)/shard_map/all_gather | solution.py:45
  887.0 15.0 %copy-start = (f32[1024,4,1024]{2,0,1:T(8,128)S(1)}, f32[1024,4,1024]{2,0,1:T(8,128)}, u32[]{:S(2)}) copy-start(f32[1024,4,1024]{2,0,1:T(8,128)} %all-gather.10.cloned.1.call-done) | copy-start | bytes 50331652
Sparse Core Ops, SparseCore 0:
  44.4 300.6 all-reduce.1
  386.1 47.5 all-gather.13
  458.5 124.9 all-gather.5
  610.7 124.6 all-gather.7
  762.3 124.6 all-gather.9
  913.8 72.4 all-gather.11
where the time goes:
time: 1020 us
  waiting for transfers between devices  782 us (77%)
  matrix products  148 us (15%)
  blocking collectives  37.3 us (4%)
  local copies, waits for them, and re-layouts  33.2 us (3%)
  between operations  15.4 us (2%)
    all_gather x4, waiting for transfers between devices, local(): whole = lax.all_gather(iterate, 'dp', axis=0, tiled=True)  422 us
    psum x1, waiting for transfers between devices, local(): lax.psum(jnp.einsum('tkr,tkc->rkc', blocks, blocks, preferred_element_typ...  301 us
    all_gather x1, waiting for transfers between devices, local(): lax.all_gather(inverse, 'dp', axis=0, tiled=True)  59.4 us
    dot_general x4, matrix products, local(): jnp.einsum('rkj,jkc->rkc', factor, whole, precision=lax.Precision.HIGHEST)  57 us
    dot_general x4, matrix products, local(): jnp.einsum('rkj,jkc->rkc', product, whole, precision=lax.Precision.HIGHEST)  48 us
    psum x1, blocking collectives, local(): block_squares = lax.psum(jnp.sum(factor * factor, axis=(0, 2)), 'dp')  31.8 us
    dot_general x1, matrix products, local(): jnp.einsum('rkc,kcf->krf', lax.all_gather(inverse, 'dp', axis=0, tiled=Tr...  25.9 us
  transfers between devices with their start and end apart: 6, of which 6 were waited for; matrix products, arithmetic and copies ran while one was open for 1% of the time, Pallas kernels for 0%

commit v1 on v0

--- a/solution.py
+++ b/solution.py
@@ -33,7 +33,15 @@
     largest = lax.pmax(jnp.max(block_squares), "tensor")
     iterate = jnp.broadcast_to(identity / jnp.sqrt(largest), factor.shape)
     for sweep in range(ITERS):
-        whole = lax.all_gather(iterate, "dp", axis=0, tiled=True)
+        whole = jnp.concatenate(
+            jax.lax.all_to_all(
+                jnp.stack([iterate for _ in range(jax.lax.axis_size("dp"))]),
+                split_axis=0,
+                concat_axis=0,
+                axis_name="dp",
+            ),
+            0,
+        )
         product = jnp.einsum("rkj,jkc->rkc", factor, whole, precision=lax.Precision.HIGHEST)
         iterate = 2.0 * iterate - jnp.einsum(
             "rkj,jkc->rkc", product, whole, precision=lax.Precision.HIGHEST

time: 1020 us -> 2100 us (2.06)
  blocking collectives: 37.3 us -> 1510 us
  waiting for transfers between devices: 782 us -> 364 us
  local copies, waits for them, and re-layouts: 33.2 us -> 71.1 us
    all_to_all x0 -> x4, blocking collectives: none -> 1470 us  [local(): jax.lax.all_to_all(jnp.stack([iterate for _ in range(jax.lax.axis_size('d...]
    all_gather x4 -> x0, waiting for transfers between devices: 422 us -> none  [local(): whole = lax.all_gather(iterate, 'dp', axis=0, tiled=True)]
    all_to_all x0 -> x4, local copies, waits for them, and re-layouts: none -> 29.4 us  [local(): jax.lax.all_to_all(jnp.stack([iterate for _ in range(jax.lax.axis_size('d...]
  transfers between devices with their start and end apart: 6 -> 2, of which waited for: 6 -> 2; matrix products, arithmetic and copies ran while one was open for 1% -> 1% of each run, Pallas kernels for 0% -> 0%
where the time goes in v1:
time: 2100 us
  blocking collectives  1510 us (72%)
  waiting for transfers between devices  364 us (17%)
  matrix products  136 us (6%)
  local copies, waits for them, and re-layouts  71.1 us (3%)
    all_to_all x4, blocking collectives, local(): jax.lax.all_to_all(jnp.stack([iterate for _ in range(jax.lax.axis_size('d...  1470 us
    psum x1, waiting for transfers between devices, local(): lax.psum(jnp.einsum('tkr,tkc->rkc', blocks, blocks, preferred_element_typ...  301 us
    all_gather x1, waiting for transfers between devices, local(): lax.all_gather(inverse, 'dp', axis=0, tiled=True)  63 us
    dot_general x4, matrix products, local(): jnp.einsum('rkj,jkc->rkc', factor, whole, precision=lax.Precision.HIGHEST)  48.4 us
    dot_general x4, matrix products, local(): jnp.einsum('rkj,jkc->rkc', product, whole, precision=lax.Precision.HIGHEST)  45.3 us
  transfers between devices with their start and end apart: 2, of which 2 were waited for; matrix products, arithmetic and copies ran while one was open for 1% of the time, Pallas kernels for 0%

profile of v1, /device:TPU:0, one launch (start us, length us, event | category | flops | bytes accessed | tf_op | source)
XLA Modules:
  0.0 2095.0 jit_solution(8938493958303505855)
XLA Ops:
  6.5 0.0 all-reduce.2.cloned.1.call-start
  7.2 7.9 constant_dynamic-slice_fusion.1
  15.1 12.0 copy.45
  27.1 17.1 convolution_bitcast_fusion
  44.2 0.0 all-reduce.2.cloned.1.call-update
  44.2 0.0 all-gather.2.cloned.1.call-start
  44.3 0.1 fusion.6
  44.4 300.7 %all-reduce.2.cloned.1.call-done = f32[1024,4,1024]{2,0,1:T(8,128)} async-done(((f32[1024,4,1024]{2,0,1:T(8,128)}), f32[1024,4,1024]{2,0,1:T(8,128)}) %all-reduce.2.cloned.1.call-update) | async-done | bytes 16777232 | tf_op jit(solution)/shard_map/psum | solution.py:24
  345.0 1.5 multiply_reduce_fusion
  346.5 31.8 %psum.15 = f32[4]{0:T(128)S(1)} all-reduce(f32[4]{0:T(128)S(1)} %multiply_reduce_fusion), channel_id=1, replica_groups=mesh['dp'=16,'tensor'=2] {'dp'}, use_global_device_ids=true, to_apply=%region_2.3 | all-reduce | flops 4 | bytes 32 | tf_op jit(solution)/shard_map/psum | solution.py:32
  378.3 0.6 reduce_max.9
  378.9 5.5 pmax.7
  385.2 0.1 broadcast_multiply_fusion
  385.3 2.1 stack.8
  387.4 365.4 %all_to_all.20 = f32[16,64,4,1024]{3,1,2,0:T(8,128)} all-to-all(f32[16,64,4,1024]{3,1,2,0:T(8,128)S(1)} %stack.8), channel_id=1, replica_groups=mesh['dp'=16,'tensor'=2] {'dp'}, dimensions={0} | all-to-all | bytes 33554432 | tf_op jit(solution)/shard_map/all_to_all | solution.py:37
  752.8 7.3 copy.39
  760.1 12.1 convolution_bitcast_fusion.8
  772.2 11.3 fusion.3
  783.5 2.1 stack.9
  785.7 367.0 %all_to_all.21 = f32[16,64,4,1024]{3,1,2,0:T(8,128)} all-to-all(f32[16,64,4,1024]{3,1,2,0:T(8,128)S(1)} %stack.9), channel_id=1, replica_groups=mesh['dp'=16,'tensor'=2] {'dp'}, dimensions={0} | all-to-all | bytes 33554432 | tf_op jit(solution)/shard_map/all_to_all | solution.py:37
  1152.7 7.3 copy.40
  1159.9 12.1 convolution_bitcast_fusion.6
  1172.0 11.1 fusion.2
  1183.1 2.1 stack.10
  1185.3 368.2 %all_to_all.22 = f32[16,64,4,1024]{3,1,2,0:T(8,128)} all-to-all(f32[16,64,4,1024]{3,1,2,0:T(8,128)S(1)} %stack.10), channel_id=1, replica_groups=mesh['dp'=16,'tensor'=2] {'dp'}, dimensions={0} | all-to-all | bytes 33554432 | tf_op jit(solution)/shard_map/all_to_all | solution.py:37
  1553.4 7.5 copy.41
  1560.9 12.1 convolution_bitcast_fusion.4
  1573.0 11.0 fusion.1
  1584.1 2.1 stack.11
  1586.2 368.2 %all_to_all.23 = f32[16,64,4,1024]{3,1,2,0:T(8,128)} all-to-all(f32[16,64,4,1024]{3,1,2,0:T(8,128)S(1)} %stack.11), channel_id=1, replica_groups=mesh['dp'=16,'tensor'=2] {'dp'}, dimensions={0} | all-to-all | bytes 33554432 | tf_op jit(solution)/shard_map/all_to_all | solution.py:37
  1954.4 7.3 copy.42
  1961.7 12.1 convolution_bitcast_fusion.2
  1973.8 11.9 fusion.4
  1985.7 0.0 all-gather.2.cloned.1.call-update
  1985.7 13.3 constant_dynamic-slice_fusion
  1999.0 63.0 %all-gather.2.cloned.1.call-done = bf16[1024,4,1024]{2,0,1:T(8,128)(2,1)} async-done(((bf16[64,4,1024]{2,0,1:T(8,128)(2,1)}), bf16[1024,4,1024]{2,0,1:T(8,128)(2,1)}) %all-gather.2.cloned.1.call-update) | async-done | bytes 8388624 | tf_op jit(solution)/shard_map/all_gather | solution.py:53
  2062.1 25.7 %fusion.7 = f32[4,1024,1792]{2,1,0:T(8,128)} fusion(bf16[1024,4,1024]{2,0,1:T(8,128)(2,1)} %all-gather.2.cloned.1.call-done, bf16[4,1024,1792]{2,1,0:T(8,128)(2,1)} %bitcast.64), kind=kOutput, calls=%fused_computation.23 | convolution fusion | flops 15032385536 | bytes 52428800 | tf_op jit(solution)/shard_map/rkc,kcf->krf/dot_general | solution.py:51
  (1 shorter events, 0.0 us)
Async XLA Ops:
  6.5 338.5 %all-reduce.2.cloned.1.call-start = ((), (), s32[]{:S(2)}) async-start(), calls=%async_computation.4 | async-start | bytes 33554432 | tf_op jit(solution)/shard_map/psum | solution.py:24
  44.2 2017.8 %all-gather.2.cloned.1.call-start = ((), (), s32[]{:S(2)}) async-start(), calls=%async_computation.5 | async-start | bytes 8912896 | tf_op jit(solution)/shard_map/all_gather | solution.py:53
Sparse Core Ops, SparseCore 0:
  44.3 300.6 all-reduce.1
  1985.9 76.1 all-gather.1
